TPU v7x, 128 devices: a whole 4x4x4 slice. The times are simulated.
128 devices in a mesh: up: 16 (over y_lo, x, core), dn: 8 (over y_hi, z).
Axes of the slice: x: 4, y: 4 (y_hi: 2, y_lo: 2; y = y_hi * 2 + y_lo), z: 4, core: 2. Of those that a mesh axis runs over, the one named last changes fastest.
Arguments:
- start_vector: bfloat16 [13312, 13312], P('up', 'dn'), may hold values from -6 to 6
- hop_tiles: bfloat16 [104, 5, 128, 128], replicated, may hold values from -0.5 to 0.5
- tile_columns: int32 [104, 5], replicated, may hold values from 0 to 103, as said below
- tile_signs: int32 [104, 5], replicated, may hold values from 0 to 1
- occupation: int32 [16, 13312], replicated, may hold values from 0 to 1, as said below
Outputs:
- next_vector: bfloat16 [13312, 13312], P('up', 'dn')
- alphas: float32 [2], replicated
- betas: float32 [2], replicated
Inputs may be any that keep to these rules, and one draw needn't show every extreme that they name: Each row of tile_columns names 5 different tile columns. Every column of occupation holds exactly 8 ones.
All inputs are finite; a program needn't handle non-finite values.
Results may differ from a plain program's by a relative error of at most 0.0065.
Values may be sent and summed in bfloat16 or wider, within the bound.
A program may use at most 192 MiB of HBM per device.

v0:
```python
import functools

import jax
import jax.numpy as jnp
from jax import lax
from jax.sharding import Mesh
from jax.sharding import PartitionSpec as P

STEPS = 2
UP = ("up_0", "up_1", "up_2")
DN = ("dn_0", "dn_1")
UP_DN = ("up_0", "up_1", "up_2", "dn_0", "dn_1")


coupling = 4.0


def split_up(value, dim, peers):
    before, after = (value.shape[:dim], value.shape[dim + 1 :])
    return jnp.moveaxis(value.reshape(*before, peers, -1, *after), dim, 0)


def joined_along(pieces, dim):
    pieces = jnp.moveaxis(pieces, 0, dim)
    shape = pieces.shape
    return pieces.reshape(*shape[:dim], shape[dim] * shape[dim + 1], *shape[dim + 2 :])


def moved_by_axis(pieces, axes, order):
    inside = pieces.shape[1:]
    whole = pieces.reshape(*(lax.axis_size(a) for a in axes), *inside)
    for k in order:
        whole = lax.all_to_all(whole, axes[k], k, k, tiled=True)
    return whole.reshape(-1, *inside)


def exchange_by_chip(value, groups, order, split_dim, concat_dim):
    peers = lax.axis_size(groups[0]) * lax.axis_size(groups[1])
    pieces = split_up(value, split_dim, peers)
    return joined_along(moved_by_axis(pieces, groups, order), concat_dim)


def edges_of(length, count):
    step = length // count
    if step >= 8:
        step -= step % 8
    return [step * k for k in range(1, count)]


def cut_exchange(value, axis, pieces, split_dim, concat_dim):
    blocks = split_up(value, split_dim, lax.axis_size(axis))
    cut = max(range(1, max(2, blocks.ndim - 1)), key=lambda d: blocks.shape[d])
    gathered = []
    for piece in jnp.split(blocks, edges_of(blocks.shape[cut], pieces), axis=cut):
        if piece.size:
            gathered.append(lax.all_to_all(piece, axis, split_axis=0, concat_axis=0, tiled=True))
    return joined_along(jnp.concatenate(gathered, axis=cut), concat_dim)


def one_axis_at_a_time(value, axes):
    return functools.reduce(lax.psum, axes, value)


def hop_lead(matrix, signed, tile_columns):
    layout = matrix.shape
    tile_width = signed.shape[-1]
    cube = matrix.reshape(layout[0] // tile_width, tile_width, -1)
    picked = cube[tile_columns]
    result = jnp.einsum("ikab,ikbm->iam", signed, picked, preferred_element_type=jnp.float32)
    return result.reshape(layout).astype(jnp.bfloat16)


def body(start_vector, hop_tiles, tile_columns, tile_signs, occupation):
    signed = hop_tiles * (1 - 2 * tile_signs).astype(jnp.bfloat16)[:, :, None, None]
    rows_local, cols_local = start_vector.shape
    count_up = lax.axis_size(UP)
    count_down = lax.axis_size(DN)
    row_start = lax.axis_index(UP) * rows_local
    col_start = lax.axis_index(DN) * cols_local
    block_rows, block_cols = start_vector.shape
    occ_rows = lax.dynamic_slice_in_dim(occupation, row_start, block_rows, 1).astype(jnp.bfloat16)
    occ_cols = lax.dynamic_slice_in_dim(occupation, col_start, block_cols, 1).astype(jnp.bfloat16)
    diagonal = coupling * jnp.einsum(
        "sa,sb->ab", occ_rows, occ_cols, preferred_element_type=jnp.float32
    )
    vector = start_vector.astype(jnp.float32)
    total = one_axis_at_a_time(jnp.sum(vector * vector), UP_DN)
    vector = vector / jnp.maximum(jnp.sqrt(total), 1.0)
    length = total / jnp.maximum(total, 1.0)
    previous = jnp.zeros_like(vector)
    beta_value = jnp.float32(0.0)
    alpha_list = []
    beta_list = []
    for iteration in range(STEPS):
        rounded = vector.astype(jnp.bfloat16)
        cube = rounded.reshape(block_rows, count_up, block_cols // count_up)
        up_part = lax.all_to_all(cube, UP, split_axis=1, concat_axis=0, tiled=True)
        up_whole = up_part.reshape(up_part.shape[0], up_part.shape[2])
        up_hopped = hop_lead(up_whole, signed, tile_columns).reshape(up_part.shape)
        moved = exchange_by_chip(up_hopped, (("up_0", "up_1"), "up_2"), (1, 0), 0, 1)
        hopped_up = moved.reshape(block_rows, block_cols)
        flipped = rounded.T.reshape(block_cols, count_down, block_rows // count_down)
        part = lax.all_to_all(flipped, DN, split_axis=1, concat_axis=0, tiled=True)
        whole = part.reshape(part.shape[0], part.shape[2])
        hopped = hop_lead(whole, signed, tile_columns).reshape(part.shape)
        returned = cut_exchange(hopped, DN, 2, 0, 1)
        hopped_down = returned.reshape(block_cols, block_rows).T
        work = (
            hopped_up.astype(jnp.float32)
            + hopped_down.astype(jnp.float32)
            + diagonal * vector
            - beta_value * previous
        )
        intersect, square = (
            one_axis_at_a_time(jnp.sum(work * vector), UP_DN),
            one_axis_at_a_time(jnp.sum(work * work), UP_DN),
        )
        work = work - intersect * vector
        residual = square - 2.0 * intersect * intersect + intersect * intersect * length
        beta_value = jnp.sqrt(jnp.maximum(residual, 1.0))
        length = residual / jnp.maximum(residual, 1.0)
        previous = vector
        vector = work / beta_value
        alpha_list.append(intersect)
        beta_list.append(beta_value)
    final = vector.astype(jnp.bfloat16)
    return (final, jnp.stack(alpha_list), jnp.stack(beta_list))


def solution(mesh):
    torus = Mesh(mesh.devices.reshape(2, 4, 2, 2, 4), ("up_0", "up_1", "up_2", "dn_0", "dn_1"))
    return jax.shard_map(
        body,
        mesh=torus,
        in_specs=(P(UP, DN), P(), P(), P(), P()),
        out_specs=(P(UP, DN), P(), P()),
        check_vma=False,
    )
```

profile of v0, /device:TPU:1, one launch (start us, length us, event | category | flops | bytes accessed | tf_op | source)
XLA Modules:
  0.0 684.3 jit_solution(5031893322592115355)
XLA Ops:
  9.5 9.2 %psum.176 = f32[]{:T(128)} all-reduce(f32[]{:T(128)} %psum.175), channel_id=1, replica_groups=mesh['up_0'=2,'up_1'=4,'up_2'=2,'dn_0'=2,'dn_1'=4] {'up_1'}, use_global_device_ids=true, to_apply=%region_2.0 | all-reduce | flops 1 | bytes 8 | tf_op jit(solution)/shard_map/psum | solution.py:61
  18.7 6.6 psum.177
  25.3 5.9 psum.178
  31.2 10.4 %psum.179 = f32[]{:T(128)} all-reduce(f32[]{:T(128)} %psum.178), channel_id=1, replica_groups=mesh['up_0'=2,'up_1'=4,'up_2'=2,'dn_0'=2,'dn_1'=4] {'dn_1'}, use_global_device_ids=true, to_apply=%region_5.0 | all-reduce | flops 1 | bytes 8 | tf_op jit(solution)/shard_map/psum | solution.py:61
  50.7 5.3 copy.58
  56.3 27.6 %all-to-all-done.3 = bf16[1664,8,104]{0,2,1:T(8,128)(2,1)S(1)} async-done(((bf16[1664,8,104]{0,2,1:T(8,128)(2,1)}), bf16[1664,8,104]{0,2,1:T(8,128)(2,1)S(1)}, u32[]{:S(2)}, u32[]{:S(2)}) %all-to-all-start.3) | async-done | bytes 2768928 | tf_op jit(solution)/shard_map/all_to_all | solution.py:103
  83.9 5.9 all-to-all-start
  91.9 6.2 reshape_reshape.9
  100.2 20.0 %gather_fusion.1 = bf16[520,128,104]{1,2,0:T(8,128)(2,1)} fusion(bf16[104,128,104]{1,2,0:T(8,128)(2,1)S(1)} %copy.67, s32[1024]{0:T(1024)S(1)} %pad_clamp_fusion), kind=kCustom, calls=%fused_computation.1 | custom fusion | bytes 27691040 | tf_op jit(solution)/shard_map/gather | solution.py:68
  120.2 13.1 %bitcast_convert_fusion.2 = bf16[104,128,104]{1,2,0:T(8,128)(2,1)S(1)} fusion(bf16[104,5,128,104]{2,3,1,0:T(8,128)(2,1)} %bitcast.104, bf16[104,5,128,128]{3,2,1,0:T(8,128)(2,1)} %param.6, bf16[104,5]{1,0:T(8,128)(2,1)S(1)} %copy.57), kind=kOutput, calls=%fused_computation.26 | convolution fusion | flops 1781997568 | bytes 33653776 | tf_op jit(solution)/shard_map/ikab,ikbm->iam/dot_general | solution.py:69
  135.2 5.2 convert_element_type.131
  152.4 20.0 %gather_fusion = bf16[520,128,104]{1,2,0:T(8,128)(2,1)} fusion(bf16[104,128,104]{1,2,0:T(8,128)(2,1)S(1)} %copy.61, s32[1024]{0:T(1024)S(1)} %pad_clamp_fusion), kind=kCustom, calls=%fused_computation | custom fusion | bytes 27691040 | tf_op jit(solution)/shard_map/gather | solution.py:68
  172.4 13.1 %bitcast_convert_fusion.3 = bf16[104,128,104]{1,2,0:T(8,128)(2,1)S(1)} fusion(bf16[104,5,128,104]{2,3,1,0:T(8,128)(2,1)} %bitcast.105, bf16[104,5,128,128]{3,2,1,0:T(8,128)(2,1)} %param.6, bf16[104,5]{1,0:T(8,128)(2,1)S(1)} %copy.57), kind=kOutput, calls=%fused_computation.27 | convolution fusion | flops 1781997568 | bytes 33653776 | tf_op jit(solution)/shard_map/ikab,ikbm->iam/dot_general | solution.py:69
  187.4 6.4 convert_element_type.125
  194.2 5.9 all_to_all.100
  207.3 17.1 %all-to-all-done.4 = bf16[8,832,1,104]{1,3,2,0:T(8,128)(2,1)} async-done(((bf16[8,832,1,104]{1,3,2,0:T(8,128)(2,1)}), bf16[8,832,1,104]{1,3,2,0:T(8,128)(2,1)}, u32[]{:S(2)}, u32[]{:S(2)}) %all-to-all-start.4) | async-done | bytes 1384480 | tf_op jit(solution)/shard_map/all_to_all | solution.py:56
  224.4 5.4 all-to-all-start.5
  234.5 15.1 %all-to-all-done.5 = bf16[8,832,1,104]{1,3,2,0:T(8,128)(2,1)} async-done(((bf16[8,832,1,104]{1,3,2,0:T(8,128)(2,1)}), bf16[8,832,1,104]{1,3,2,0:T(8,128)(2,1)}, u32[]{:S(2)}, u32[]{:S(2)}) %all-to-all-start.5) | async-done | bytes 1384480 | tf_op jit(solution)/shard_map/all_to_all | solution.py:56
  255.6 5.1 maximum_convert_fusion
  260.7 30.2 %all-to-all-done.2 = bf16[8,2,832,1,104]{2,1,4,3,0:T(2,128)(2,1)S(1)} async-done(((bf16[8,2,832,1,104]{2,1,4,3,0:T(2,128)(2,1)}), bf16[8,2,832,1,104]{2,1,4,3,0:T(2,128)(2,1)S(1)}, u32[]{:S(2)}, u32[]{:S(2)}) %all-to-all-start.2) | async-done | bytes 2768928 | tf_op jit(solution)/shard_map/all_to_all | solution.py:33
  294.4 7.2 %copy.71 = f32[832,1664]{1,0:T(8,128)} copy(f32[832,1664]{0,1:T(8,128)} %bitcast.101) | data formatting | bytes 11075584 | tf_op jit(solution)/shard_map/convert_element_type | solution.py:109
  301.6 11.1 %multiply_reduce_fusion.3 = (f32[]{:T(128)}, f32[]{:T(128)}, f32[832,1664]{1,0:T(8,128)}, f32[832,1664]{1,0:T(8,128)}) fusion(f32[]{:T(128)S(6)} %max.13, bf16[832,1664]{1,0:T(8,128)(2,1)S(1)} %copy-done, f32[832,1664]{1,0:T(8,128)} %copy.71, f32[8,1664,1,104]{1,3,2,0:T(8,128)} %maximum_convert_fusion, s32[16,13312]{1,0:T(8,128)} %param.9, ...), kind=kOutput, calls=%fused_computation.33 | convolution fusion | flops 58186752 | bytes 25083924 | tf_op jit(solution)/shard_map/sa,sb->ab/dot_general | solution.py:83
  317.1 10.7 %all-reduce.3 = (f32[]{:T(128)}, f32[]{:T(128)}) all-reduce(f32[]{:T(128)} %get-tuple-element.25, f32[]{:T(128)} %get-tuple-element.26), channel_id=1, replica_groups=mesh['up_0'=2,'up_1'=4,'up_2'=2,'dn_0'=2,'dn_1'=4] {'up_1'}, use_global_device_ids=true, to_apply=%region_14.0 | all-reduce | flops 2 | bytes 16 | tf_op jit(solution)/shard_map/psum | solution.py:61
  327.8 8.6 %all-reduce.7 = (f32[]{:T(128)}, f32[]{:T(128)}) all-reduce(f32[]{:T(128)} %get-tuple-element.13, f32[]{:T(128)} %get-tuple-element.14), channel_id=1, replica_groups=mesh['up_0'=2,'up_1'=4,'up_2'=2,'dn_0'=2,'dn_1'=4] {'up_2'}, use_global_device_ids=true, to_apply=%region_15.0 | all-reduce | flops 2 | bytes 16 | tf_op jit(solution)/shard_map/psum | solution.py:61
  336.4 9.0 %all-reduce.5 = (f32[]{:T(128)}, f32[]{:T(128)}) all-reduce(f32[]{:T(128)} %get-tuple-element.21, f32[]{:T(128)} %get-tuple-element.22), channel_id=1, replica_groups=mesh['up_0'=2,'up_1'=4,'up_2'=2,'dn_0'=2,'dn_1'=4] {'dn_0'}, use_global_device_ids=true, to_apply=%region_16.0 | all-reduce | flops 2 | bytes 16 | tf_op jit(solution)/shard_map/psum | solution.py:61
  345.4 9.1 %all-reduce.1 = (f32[]{:T(128)}, f32[]{:T(128)}) all-reduce(f32[]{:T(128)} %get-tuple-element.17, f32[]{:T(128)} %get-tuple-element.18), channel_id=1, replica_groups=mesh['up_0'=2,'up_1'=4,'up_2'=2,'dn_0'=2,'dn_1'=4] {'dn_1'}, use_global_device_ids=true, to_apply=%region_17.0 | all-reduce | flops 2 | bytes 16 | tf_op jit(solution)/shard_map/psum | solution.py:61
  357.9 7.6 %fusion.28 = (bf16[832,1664]{1,0:T(8,128)(2,1)}, f32[832,1664]{1,0:T(8,128)}) fusion(f32[]{:T(128)} %sqrt.10, f32[832,1664]{1,0:T(8,128)} %get-tuple-element.30, f32[]{:T(128)S(6)} %max.13, bf16[832,1664]{1,0:T(8,128)(2,1)S(1)} %copy-done, f32[]{:T(128)} %get-tuple-element.10), kind=kLoop, calls=%fused_computation.48 | loop fusion | flops 8306688 | bytes 16613388 | tf_op jit(solution)/shard_map/convert_element_type | solution.py:95
  373.9 29.8 %all-to-all-done.9 = bf16[1664,8,104]{0,2,1:T(8,128)(2,1)} async-done(((bf16[1664,8,104]{0,2,1:T(8,128)(2,1)}), bf16[1664,8,104]{0,2,1:T(8,128)(2,1)}, u32[]{:S(2)}, u32[]{:S(2)}) %all-to-all-start.9) | async-done | bytes 2768928 | tf_op jit(solution)/shard_map/all_to_all | solution.py:103
  403.7 5.8 all-to-all-start.6
  417.8 20.0 %gather_fusion.3 = bf16[520,128,104]{1,2,0:T(8,128)(2,1)} fusion(bf16[104,128,104]{1,2,0:T(8,128)(2,1)S(1)} %copy.80, s32[1024]{0:T(1024)S(1)} %pad_clamp_fusion), kind=kCustom, calls=%fused_computation.3 | custom fusion | bytes 27691040 | tf_op jit(solution)/shard_map/gather | solution.py:68
  437.8 13.1 %bitcast_convert_fusion = bf16[104,128,104]{1,2,0:T(8,128)(2,1)S(1)} fusion(bf16[104,5,128,104]{2,3,1,0:T(8,128)(2,1)} %bitcast.106, bf16[104,5,128,128]{3,2,1,0:T(8,128)(2,1)} %param.6, bf16[104,5]{1,0:T(8,128)(2,1)S(1)} %copy.57), kind=kOutput, calls=%fused_computation.24 | convolution fusion | flops 1781997568 | bytes 33653776 | tf_op jit(solution)/shard_map/ikab,ikbm->iam/dot_general | solution.py:69
  452.8 5.2 convert_element_type.146
  469.9 20.0 %gather_fusion.2 = bf16[520,128,104]{1,2,0:T(8,128)(2,1)} fusion(bf16[104,128,104]{1,2,0:T(8,128)(2,1)S(1)} %copy.74, s32[1024]{0:T(1024)S(1)} %pad_clamp_fusion), kind=kCustom, calls=%fused_computation.2 | custom fusion | bytes 27691040 | tf_op jit(solution)/shard_map/gather | solution.py:68
  489.8 13.1 %bitcast_convert_fusion.1 = bf16[104,128,104]{1,2,0:T(8,128)(2,1)S(1)} fusion(bf16[104,5,128,104]{2,3,1,0:T(8,128)(2,1)} %bitcast.103, bf16[104,5,128,128]{3,2,1,0:T(8,128)(2,1)} %param.6, bf16[104,5]{1,0:T(8,128)(2,1)S(1)} %copy.57), kind=kOutput, calls=%fused_computation.25 | convolution fusion | flops 1781997568 | bytes 33653776 | tf_op jit(solution)/shard_map/ikab,ikbm->iam/dot_general | solution.py:69
  504.8 6.4 convert_element_type.140
  511.6 5.9 all_to_all.101
  524.7 17.1 %all-to-all-done.10 = bf16[8,832,1,104]{1,3,2,0:T(8,128)(2,1)} async-done(((bf16[8,832,1,104]{1,3,2,0:T(8,128)(2,1)}), bf16[8,832,1,104]{1,3,2,0:T(8,128)(2,1)}, u32[]{:S(2)}, u32[]{:S(2)}) %all-to-all-start.10) | async-done | bytes 1384480 | tf_op jit(solution)/shard_map/all_to_all | solution.py:56
  541.8 5.4 all-to-all-start.11
  551.9 15.1 %all-to-all-done.11 = bf16[8,832,1,104]{1,3,2,0:T(8,128)(2,1)} async-done(((bf16[8,832,1,104]{1,3,2,0:T(8,128)(2,1)}), bf16[8,832,1,104]{1,3,2,0:T(8,128)(2,1)}, u32[]{:S(2)}, u32[]{:S(2)}) %all-to-all-start.11) | async-done | bytes 1384480 | tf_op jit(solution)/shard_map/all_to_all | solution.py:56
  571.8 5.1 maximum_convert_fusion.1
  576.8 31.5 %all-to-all-done.8 = bf16[8,2,832,1,104]{2,1,4,3,0:T(2,128)(2,1)S(1)} async-done(((bf16[8,2,832,1,104]{2,1,4,3,0:T(2,128)(2,1)}), bf16[8,2,832,1,104]{2,1,4,3,0:T(2,128)(2,1)S(1)}, u32[]{:S(2)}, u32[]{:S(2)}) %all-to-all-start.8) | async-done | bytes 2768928 | tf_op jit(solution)/shard_map/all_to_all | solution.py:33
  611.8 7.2 %copy.84 = f32[832,1664]{1,0:T(8,128)} copy(f32[832,1664]{0,1:T(8,128)} %bitcast.102) | data formatting | bytes 11075584 | tf_op jit(solution)/shard_map/convert_element_type | solution.py:109
  619.0 11.7 %multiply_reduce_fusion.1 = (f32[]{:T(128)}, f32[]{:T(128)}, f32[832,1664]{1,0:T(8,128)}) fusion(f32[832,1664]{1,0:T(8,128)} %get-tuple-element.29, f32[]{:T(128)S(6)} %max.13, bf16[832,1664]{1,0:T(8,128)(2,1)S(1)} %copy-done.1, f32[]{:T(128)} %sqrt.10, f32[832,1664]{1,0:T(8,128)} %get-tuple-element.35, f32[832,1664]{1,0:T(8,128)} %copy.84, ...), kind=kLoop, calls=%fused_computation.30 | loop fusion | flops 16613374 | bytes 30457872 | tf_op jit(solution)/shard_map/reduce_sum | solution.py:115
  635.1 10.7 %all-reduce.2 = (f32[]{:T(128)}, f32[]{:T(128)}) all-reduce(f32[]{:T(128)} %get-tuple-element.23, f32[]{:T(128)} %get-tuple-element.24), channel_id=1, replica_groups=mesh['up_0'=2,'up_1'=4,'up_2'=2,'dn_0'=2,'dn_1'=4] {'up_1'}, use_global_device_ids=true, to_apply=%region_26.0 | all-reduce | flops 2 | bytes 16 | tf_op jit(solution)/shard_map/psum | solution.py:61
  645.8 8.6 %all-reduce.6 = (f32[]{:T(128)}, f32[]{:T(128)}) all-reduce(f32[]{:T(128)} %get-tuple-element.11, f32[]{:T(128)} %get-tuple-element.12), channel_id=1, replica_groups=mesh['up_0'=2,'up_1'=4,'up_2'=2,'dn_0'=2,'dn_1'=4] {'up_2'}, use_global_device_ids=true, to_apply=%region_27.0 | all-reduce | flops 2 | bytes 16 | tf_op jit(solution)/shard_map/psum | solution.py:61
  654.4 9.1 %all-reduce.4 = (f32[]{:T(128)}, f32[]{:T(128)}) all-reduce(f32[]{:T(128)} %get-tuple-element.19, f32[]{:T(128)} %get-tuple-element.20), channel_id=1, replica_groups=mesh['up_0'=2,'up_1'=4,'up_2'=2,'dn_0'=2,'dn_1'=4] {'dn_0'}, use_global_device_ids=true, to_apply=%region_28.0 | all-reduce | flops 2 | bytes 16 | tf_op jit(solution)/shard_map/psum | solution.py:61
  663.4 9.0 %all-reduce = (f32[]{:T(128)}, f32[]{:T(128)}) all-reduce(f32[]{:T(128)} %get-tuple-element.15, f32[]{:T(128)} %get-tuple-element.16), channel_id=1, replica_groups=mesh['up_0'=2,'up_1'=4,'up_2'=2,'dn_0'=2,'dn_1'=4] {'dn_1'}, use_global_device_ids=true, to_apply=%region_29.0 | all-reduce | flops 2 | bytes 16 | tf_op jit(solution)/shard_map/psum | solution.py:61
  675.3 7.0 %divide_convert_fusion = bf16[832,1664]{1,0:T(8,128)(2,1)} fusion(f32[832,1664]{1,0:T(8,128)} %get-tuple-element.27, f32[832,1664]{1,0:T(8,128)} %get-tuple-element.29, f32[]{:T(128)} %sqrt.11, f32[]{:T(128)} %get-tuple-element.8), kind=kLoop, calls=%fused_computation.28 | loop fusion | flops 5537792 | bytes 13844488 | tf_op jit(solution)/shard_map/convert_element_type | solution.py:126
  (60 shorter events, 121.5 us)
Async XLA Ops:
  46.1 10.0 %copy-start.4 = (s32[104,5]{0,1:T(8,128)S(1)}, s32[104,5]{0,1:T(8,128)}, u32[]{:S(2)}) copy-start(s32[104,5]{0,1:T(8,128)} %param.7) | copy-start | bytes 6244
  46.1 10.3 %copy-start.3 = (s32[104,5]{0,1:T(8,128)S(1)}, s32[104,5]{0,1:T(8,128)}, u32[]{:S(2)}) copy-start(s32[104,5]{0,1:T(8,128)} %param.8) | copy-start | bytes 6244
  46.1 37.9 %all-to-all-start.3 = ((bf16[1664,8,104]{0,2,1:T(8,128)(2,1)}), bf16[1664,8,104]{0,2,1:T(8,128)(2,1)S(1)}, u32[]{:S(2)}, u32[]{:S(2)}) async-start(bf16[1664,8,104]{0,2,1:T(8,128)(2,1)} %bitcast.10), calls=%async_computation.3 | async-start | bytes 5537792 | tf_op jit(solution)/shard_map/all_to_all | solution.py:103
  83.9 59.6 %all-to-all-start = ((bf16[832,16,104]{0,2,1:T(8,128)(2,1)}), bf16[832,16,104]{0,2,1:T(8,128)(2,1)}, u32[]{:S(2)}, u32[]{:S(2)}) async-start(bf16[832,16,104]{0,2,1:T(8,128)(2,1)} %bitcast), calls=%async_computation | async-start | bytes 5963776 | tf_op jit(solution)/shard_map/all_to_all | solution.py:97
  200.1 24.3 %all-to-all-start.4 = ((bf16[8,832,1,104]{1,3,2,0:T(8,128)(2,1)}), bf16[8,832,1,104]{1,3,2,0:T(8,128)(2,1)}, u32[]{:S(2)}, u32[]{:S(2)}) async-start(bf16[8,832,1,104]{1,3,2,0:T(8,128)(2,1)} %copy.69), calls=%async_computation.4 | async-start | bytes 2981888 | tf_op jit(solution)/shard_map/all_to_all | solution.py:56
  224.4 25.2 %all-to-all-start.5 = ((bf16[8,832,1,104]{1,3,2,0:T(8,128)(2,1)}), bf16[8,832,1,104]{1,3,2,0:T(8,128)(2,1)}, u32[]{:S(2)}, u32[]{:S(2)}) async-start(bf16[8,832,1,104]{1,3,2,0:T(8,128)(2,1)} %copy.70), calls=%async_computation.5 | async-start | bytes 2981888 | tf_op jit(solution)/shard_map/all_to_all | solution.py:56
  249.6 41.3 %all-to-all-start.2 = ((bf16[8,2,832,1,104]{2,1,4,3,0:T(2,128)(2,1)}), bf16[8,2,832,1,104]{2,1,4,3,0:T(2,128)(2,1)S(1)}, u32[]{:S(2)}, u32[]{:S(2)}) async-start(bf16[8,2,832,1,104]{2,1,4,3,0:T(2,128)(2,1)} %copy.64), calls=%async_computation.2 | async-start | bytes 5963776 | tf_op jit(solution)/shard_map/all_to_all | solution.py:33
  294.4 7.2 %copy-start = (bf16[832,1664]{1,0:T(8,128)(2,1)S(1)}, bf16[832,1664]{1,0:T(8,128)(2,1)}, u32[]{:S(2)}) copy-start(bf16[832,1664]{1,0:T(8,128)(2,1)} %param.5) | copy-start | bytes 8306692
  365.5 4.8 copy-start.2
  365.5 38.2 %all-to-all-start.9 = ((bf16[1664,8,104]{0,2,1:T(8,128)(2,1)}), bf16[1664,8,104]{0,2,1:T(8,128)(2,1)}, u32[]{:S(2)}, u32[]{:S(2)}) async-start(bf16[1664,8,104]{0,2,1:T(8,128)(2,1)} %bitcast.100), calls=%async_computation.9 | async-start | bytes 5537792 | tf_op jit(solution)/shard_map/all_to_all | solution.py:103
  403.7 57.4 %all-to-all-start.6 = ((bf16[832,16,104]{0,2,1:T(8,128)(2,1)}), bf16[832,16,104]{0,2,1:T(8,128)(2,1)}, u32[]{:S(2)}, u32[]{:S(2)}) async-start(bf16[832,16,104]{0,2,1:T(8,128)(2,1)} %bitcast.107), calls=%async_computation.6 | async-start | bytes 5963776 | tf_op jit(solution)/shard_map/all_to_all | solution.py:97
  517.5 24.3 %all-to-all-start.10 = ((bf16[8,832,1,104]{1,3,2,0:T(8,128)(2,1)}), bf16[8,832,1,104]{1,3,2,0:T(8,128)(2,1)}, u32[]{:S(2)}, u32[]{:S(2)}) async-start(bf16[8,832,1,104]{1,3,2,0:T(8,128)(2,1)} %copy.82), calls=%async_computation.10 | async-start | bytes 2981888 | tf_op jit(solution)/shard_map/all_to_all | solution.py:56
  541.8 25.2 %all-to-all-start.11 = ((bf16[8,832,1,104]{1,3,2,0:T(8,128)(2,1)}), bf16[8,832,1,104]{1,3,2,0:T(8,128)(2,1)}, u32[]{:S(2)}, u32[]{:S(2)}) async-start(bf16[8,832,1,104]{1,3,2,0:T(8,128)(2,1)} %copy.83), calls=%async_computation.11 | async-start | bytes 2981888 | tf_op jit(solution)/shard_map/all_to_all | solution.py:56
  567.0 41.3 %all-to-all-start.8 = ((bf16[8,2,832,1,104]{2,1,4,3,0:T(2,128)(2,1)}), bf16[8,2,832,1,104]{2,1,4,3,0:T(2,128)(2,1)S(1)}, u32[]{:S(2)}, u32[]{:S(2)}) async-start(bf16[8,2,832,1,104]{2,1,4,3,0:T(2,128)(2,1)} %copy.77), calls=%async_computation.8 | async-start | bytes 5963776 | tf_op jit(solution)/shard_map/all_to_all | solution.py:33
  611.8 7.2 %copy-start.1 = (bf16[832,1664]{1,0:T(8,128)(2,1)S(1)}, bf16[832,1664]{1,0:T(8,128)(2,1)}, u32[]{:S(2)}) copy-start(bf16[832,1664]{1,0:T(8,128)(2,1)} %param.5) | copy-start | bytes 8306692
where the time goes:
time: 692 us; the launch traced here: 684 us
  local copies, waits for them, and re-layouts  193 us (28%)
  waiting for transfers between devices  184 us (27%)
  blocking collectives  132 us (19%)
  matrix products  63.4 us (9%)
  other arithmetic  52.2 us (8%)
  starting transfers between devices  50.4 us (7%)
  between operations  9.49 us (1%)
    psum x15, blocking collectives, one_axis_at_a_time(): return functools.reduce(lax.psum, axes, value)  121 us
    gather x4, local copies, waits for them, and re-layouts, hop_lead(): picked = cube[tile_columns]  79.9 us
    all_to_all x4, waiting for transfers between devices, cut_exchange(): lax.all_to_all(piece, axis, split_axis=0, concat_axis=0, tiled=True)  64.5 us
    all_to_all x2, waiting for transfers between devices, moved_by_axis(): whole = lax.all_to_all(whole, axes[k], k, k, tiled=True)  61.7 us
    all_to_all x2, waiting for transfers between devices, body(): part = lax.all_to_all(flipped, DN, split_axis=1, concat_axis=0, tiled=True)  57.4 us
    dot_general x4, matrix products, hop_lead(): jnp.einsum('ikab,ikbm->iam', signed, picked, preferred_element_type=jnp.f...  52.3 us
    convert_element_type x10, local copies, waits for them, and re-layouts, hop_lead(): return result.reshape(layout).astype(jnp.bfloat16)  31.5 us
    another operation x8, local copies, waits for them, and re-layouts, hop_lead(): cube = matrix.reshape(layout[0] // tile_width, tile_width, -1)  27.8 us
  transfers between devices with their start and end apart: 10, of which 8 were waited for; matrix products, arithmetic and copies ran while one was open for 20% of the time, Pallas kernels for 0%

commit v1 on v0

--- a/solution.py
+++ b/solution.py
@@ -3,6 +3,8 @@
 import jax
 import jax.numpy as jnp
 from jax import lax
+from jax.experimental import pallas as pl
+from jax.experimental.pallas import tpu as pltpu
 from jax.sharding import Mesh
 from jax.sharding import PartitionSpec as P
 
@@ -57,8 +59,64 @@
     return joined_along(jnp.concatenate(gathered, axis=cut), concat_dim)
 
 
-def one_axis_at_a_time(value, axes):
-    return functools.reduce(lax.psum, axes, value)
+MESH_ID = pl.DeviceIdType.MESH
+
+
+def coords(index):
+    return (index // 64, lax.rem(index // 16, 4), lax.rem(index // 8, 2), lax.rem(index // 4, 2), lax.rem(index, 4))
+
+
+def sum_kernel(x_ref, o_ref, src, dst, send_sem, recv_sem):
+    count = dst.shape[0]
+    me = lax.axis_index(UP_DN)
+    barrier = pltpu.get_barrier_semaphore()
+
+    def greet(s, carry):
+        pl.semaphore_signal(barrier, inc=1, device_id=coords(lax.rem(me + s, count)), device_id_type=MESH_ID)
+        return carry
+
+    lax.fori_loop(1, count, greet, 0)
+    src[...] = x_ref[...]
+    dst[pl.ds(me, 1)] = x_ref[...].reshape((1, *x_ref.shape))
+    pl.semaphore_wait(barrier, count - 1)
+
+    def send(s, carry):
+        pltpu.make_async_remote_copy(
+            src_ref=src,
+            dst_ref=dst.at[me],
+            send_sem=send_sem,
+            recv_sem=recv_sem,
+            device_id=coords(lax.rem(me + s, count)),
+            device_id_type=MESH_ID,
+        ).start()
+        return carry
+
+    lax.fori_loop(1, count, send, 0)
+    rest = dst.at[pl.ds(0, count - 1)]
+    whole = pltpu.make_async_remote_copy(
+        src_ref=rest, dst_ref=rest, send_sem=send_sem, recv_sem=recv_sem, device_id=coords(me), device_id_type=MESH_ID
+    )
+    whole.wait_recv()
+    whole.wait_send()
+    o_ref[...] = jnp.sum(dst[...], axis=0)
+
+
+def summed(values):
+    rows = jnp.stack([jnp.broadcast_to(v, (128,)) for v in values] + [jnp.zeros((128,), jnp.float32)] * (8 - len(values)))
+    out = pl.pallas_call(
+        sum_kernel,
+        out_shape=jax.ShapeDtypeStruct((8, 128), jnp.float32),
+        in_specs=[pl.BlockSpec(memory_space=pltpu.VMEM)],
+        out_specs=pl.BlockSpec(memory_space=pltpu.VMEM),
+        scratch_shapes=[
+            pltpu.VMEM((8, 128), jnp.float32),
+            pltpu.VMEM((128, 8, 128), jnp.float32),
+            pltpu.SemaphoreType.DMA,
+            pltpu.SemaphoreType.DMA,
+        ],
+        compiler_params=pltpu.CompilerParams(collective_id=0, has_side_effects=True),
+    )(rows)
+    return [out[k, 0] for k in range(len(values))]
 
 
 def hop_lead(matrix, signed, tile_columns):
@@ -84,7 +142,7 @@
         "sa,sb->ab", occ_rows, occ_cols, preferred_element_type=jnp.float32
     )
     vector = start_vector.astype(jnp.float32)
-    total = one_axis_at_a_time(jnp.sum(vector * vector), UP_DN)
+    (total,) = summed([jnp.sum(vector * vector)])
     vector = vector / jnp.maximum(jnp.sqrt(total), 1.0)
     length = total / jnp.maximum(total, 1.0)
     previous = jnp.zeros_like(vector)
@@ -111,10 +169,7 @@
             + diagonal * vector
             - beta_value * previous
         )
-        intersect, square = (
-            one_axis_at_a_time(jnp.sum(work * vector), UP_DN),
-            one_axis_at_a_time(jnp.sum(work * work), UP_DN),
-        )
+        intersect, square = summed([jnp.sum(work * vector), jnp.sum(work * work)])
         work = work - intersect * vector
         residual = square - 2.0 * intersect * intersect + intersect * intersect * length
         beta_value = jnp.sqrt(jnp.maximum(residual, 1.0))

time: 692 us -> 661 us (0.955)
  blocking collectives: 132 us -> 11.7 us
  Pallas kernels: 0 us -> 80.9 us
    psum x15 -> x0, blocking collectives: 121 us -> none  [one_axis_at_a_time(): return functools.reduce(lax.psum, axes, value)]
    pallas_call x0 -> x3, Pallas kernels: none -> 80.9 us  [summed(): pl.pallas_call(sum_kernel, out_shape=jax.ShapeDtypeStruct((8, 128), jnp.f...]
  transfers between devices with their start and end apart: 10 -> 10, of which waited for: 8 -> 8; matrix products, arithmetic and copies ran while one was open for 20% -> 21% of each run, Pallas kernels for 0% -> 0%
where the time goes in v1:
time: 661 us; the launch traced here: 656 us
  local copies, waits for them, and re-layouts  199 us (30%)
  waiting for transfers between devices  184 us (28%)
  Pallas kernels  80.9 us (12%)
  matrix products  63.5 us (10%)
  other arithmetic  56 us (8%)
  starting transfers between devices  51.6 us (8%)
  blocking collectives  11.7 us (2%)
  between operations  9.96 us (2%)
    pallas_call x3, Pallas kernels, summed(): pl.pallas_call(sum_kernel, out_shape=jax.ShapeDtypeStruct((8, 128), jnp.f...  80.9 us
    gather x4, local copies, waits for them, and re-layouts, hop_lead(): picked = cube[tile_columns]  79.9 us
    all_to_all x4, waiting for transfers between devices, cut_exchange(): lax.all_to_all(piece, axis, split_axis=0, concat_axis=0, tiled=True)  64.5 us
    all_to_all x2, waiting for transfers between devices, moved_by_axis(): whole = lax.all_to_all(whole, axes[k], k, k, tiled=True)  61.7 us
    all_to_all x2, waiting for transfers between devices, body(): part = lax.all_to_all(flipped, DN, split_axis=1, concat_axis=0, tiled=True)  57.7 us
    dot_general x4, matrix products, hop_lead(): jnp.einsum('ikab,ikbm->iam', signed, picked, preferred_element_type=jnp.f...  52.3 us
    convert_element_type x10, local copies, waits for them, and re-layouts, hop_lead(): return result.reshape(layout).astype(jnp.bfloat16)  31.5 us
    another operation x8, local copies, waits for them, and re-layouts, hop_lead(): cube = matrix.reshape(layout[0] // tile_width, tile_width, -1)  27.8 us
  transfers between devices with their start and end apart: 10, of which 8 were waited for; matrix products, arithmetic and copies ran while one was open for 21% of the time, Pallas kernels for 0%

profile of v1, /device:TPU:1, one launch (start us, length us, event | category | flops | bytes accessed | tf_op | source)
XLA Modules:
  0.0 656.3 jit_solution(4702270134795196362)
XLA Ops:
  5.8 23.5 %shard_map.76 = f32[8,128]{1,0:T(8,128)} custom-call(f32[8,128]{1,0:T(8,128)} %broadcast.35.x_ref), custom_call_target="tpu_custom_call" | custom-call | tf_op jit(solution)/shard_map/pallas_call | solution.py:106
  35.1 5.6 all-to-all-start.3
  40.7 5.3 copy.58
  46.3 27.7 %all-to-all-done.3 = bf16[1664,8,104]{0,2,1:T(8,128)(2,1)S(1)} async-done(((bf16[1664,8,104]{0,2,1:T(8,128)(2,1)}), bf16[1664,8,104]{0,2,1:T(8,128)(2,1)S(1)}, u32[]{:S(2)}, u32[]{:S(2)}) %all-to-all-start.3) | async-done | bytes 2768928 | tf_op jit(solution)/shard_map/all_to_all | solution.py:161
  74.1 5.8 all-to-all-start
  81.9 6.2 reshape_reshape.9
  90.2 20.0 %gather_fusion.1 = bf16[520,128,104]{1,2,0:T(8,128)(2,1)} fusion(bf16[104,128,104]{1,2,0:T(8,128)(2,1)S(1)} %copy.67, s32[1024]{0:T(1024)S(1)} %pad_clamp_fusion), kind=kCustom, calls=%fused_computation.1 | custom fusion | bytes 27691040 | tf_op jit(solution)/shard_map/gather | solution.py:126
  110.2 13.1 %bitcast_convert_fusion.2 = bf16[104,128,104]{1,2,0:T(8,128)(2,1)S(1)} fusion(bf16[104,5,128,104]{2,3,1,0:T(8,128)(2,1)} %bitcast.115, bf16[104,5,128,128]{3,2,1,0:T(8,128)(2,1)} %param.6, bf16[104,5]{1,0:T(8,128)(2,1)S(1)} %copy.57), kind=kOutput, calls=%fused_computation.26 | convolution fusion | flops 1781997568 | bytes 33653776 | tf_op jit(solution)/shard_map/ikab,ikbm->iam/dot_general | solution.py:127
  125.2 5.2 convert_element_type.131
  135.8 4.6 reshape_reshape.8
  142.5 20.0 %gather_fusion = bf16[520,128,104]{1,2,0:T(8,128)(2,1)} fusion(bf16[104,128,104]{1,2,0:T(8,128)(2,1)S(1)} %copy.61, s32[1024]{0:T(1024)S(1)} %pad_clamp_fusion), kind=kCustom, calls=%fused_computation | custom fusion | bytes 27691040 | tf_op jit(solution)/shard_map/gather | solution.py:126
  162.4 13.1 %bitcast_convert_fusion.3 = bf16[104,128,104]{1,2,0:T(8,128)(2,1)S(1)} fusion(bf16[104,5,128,104]{2,3,1,0:T(8,128)(2,1)} %bitcast.116, bf16[104,5,128,128]{3,2,1,0:T(8,128)(2,1)} %param.6, bf16[104,5]{1,0:T(8,128)(2,1)S(1)} %copy.57), kind=kOutput, calls=%fused_computation.27 | convolution fusion | flops 1781997568 | bytes 33653776 | tf_op jit(solution)/shard_map/ikab,ikbm->iam/dot_general | solution.py:127
  177.4 6.4 convert_element_type.125
  184.3 5.8 all_to_all.100
  190.1 4.5 all-to-all-start.4
  197.3 17.1 %all-to-all-done.4 = bf16[8,832,1,104]{1,3,2,0:T(8,128)(2,1)} async-done(((bf16[8,832,1,104]{1,3,2,0:T(8,128)(2,1)}), bf16[8,832,1,104]{1,3,2,0:T(8,128)(2,1)}, u32[]{:S(2)}, u32[]{:S(2)}) %all-to-all-start.4) | async-done | bytes 1384480 | tf_op jit(solution)/shard_map/all_to_all | solution.py:58
  214.4 5.4 all-to-all-start.5
  219.8 4.7 copy.64
  224.5 15.1 %all-to-all-done.5 = bf16[8,832,1,104]{1,3,2,0:T(8,128)(2,1)} async-done(((bf16[8,832,1,104]{1,3,2,0:T(8,128)(2,1)}), bf16[8,832,1,104]{1,3,2,0:T(8,128)(2,1)}, u32[]{:S(2)}, u32[]{:S(2)}) %all-to-all-start.5) | async-done | bytes 1384480 | tf_op jit(solution)/shard_map/all_to_all | solution.py:58
  239.6 4.7 all-to-all-start.2
  245.6 5.1 maximum_convert_fusion
  250.6 30.2 %all-to-all-done.2 = bf16[8,2,832,1,104]{2,1,4,3,0:T(2,128)(2,1)S(1)} async-done(((bf16[8,2,832,1,104]{2,1,4,3,0:T(2,128)(2,1)}), bf16[8,2,832,1,104]{2,1,4,3,0:T(2,128)(2,1)S(1)}, u32[]{:S(2)}, u32[]{:S(2)}) %all-to-all-start.2) | async-done | bytes 2768928 | tf_op jit(solution)/shard_map/all_to_all | solution.py:35
  284.4 7.1 %copy.71 = f32[832,1664]{1,0:T(8,128)} copy(f32[832,1664]{0,1:T(8,128)} %bitcast.112) | data formatting | bytes 11075584 | tf_op jit(solution)/shard_map/convert_element_type | solution.py:167
  291.5 11.2 %multiply_reduce_fusion.3 = (f32[]{:T(128)}, f32[]{:T(128)}, f32[832,1664]{1,0:T(8,128)}, f32[832,1664]{1,0:T(8,128)}) fusion(f32[]{:T(128)S(6)} %max.13, bf16[832,1664]{1,0:T(8,128)(2,1)S(1)} %copy-done, f32[832,1664]{1,0:T(8,128)} %copy.71, f32[8,1664,1,104]{1,3,2,0:T(8,128)} %maximum_convert_fusion, s32[16,13312]{1,0:T(8,128)} %param.9, ...), kind=kOutput, calls=%fused_computation.33 | convolution fusion | flops 58186752 | bytes 25083924 | tf_op jit(solution)/shard_map/sa,sb->ab/dot_general | solution.py:141
  304.7 28.7 %shard_map.77 = f32[8,128]{1,0:T(8,128)} custom-call(f32[8,128]{1,0:T(8,128)} %broadcast.40.x_ref), custom_call_target="tpu_custom_call" | custom-call | tf_op jit(solution)/shard_map/pallas_call | solution.py:106
  338.2 7.6 %fusion.28 = (bf16[832,1664]{1,0:T(8,128)(2,1)}, f32[832,1664]{1,0:T(8,128)}) fusion(f32[]{:T(128)} %sqrt.10, f32[832,1664]{1,0:T(8,128)} %get-tuple-element.10, f32[]{:T(128)S(6)} %max.13, bf16[832,1664]{1,0:T(8,128)(2,1)S(1)} %copy-done, f32[]{:T(128)} %bitcast.20), kind=kLoop, calls=%fused_computation.54 | loop fusion | flops 8306688 | bytes 16613388 | tf_op jit(solution)/shard_map/convert_element_type | solution.py:153
  345.9 5.3 all-to-all-start.9
  354.7 29.9 %all-to-all-done.9 = bf16[1664,8,104]{0,2,1:T(8,128)(2,1)} async-done(((bf16[1664,8,104]{0,2,1:T(8,128)(2,1)}), bf16[1664,8,104]{0,2,1:T(8,128)(2,1)}, u32[]{:S(2)}, u32[]{:S(2)}) %all-to-all-start.9) | async-done | bytes 2768928 | tf_op jit(solution)/shard_map/all_to_all | solution.py:161
  384.6 5.7 all-to-all-start.6
  398.6 20.0 %gather_fusion.3 = bf16[520,128,104]{1,2,0:T(8,128)(2,1)} fusion(bf16[104,128,104]{1,2,0:T(8,128)(2,1)S(1)} %copy.80, s32[1024]{0:T(1024)S(1)} %pad_clamp_fusion), kind=kCustom, calls=%fused_computation.3 | custom fusion | bytes 27691040 | tf_op jit(solution)/shard_map/gather | solution.py:126
  418.6 13.1 %bitcast_convert_fusion = bf16[104,128,104]{1,2,0:T(8,128)(2,1)S(1)} fusion(bf16[104,5,128,104]{2,3,1,0:T(8,128)(2,1)} %bitcast.117, bf16[104,5,128,128]{3,2,1,0:T(8,128)(2,1)} %param.6, bf16[104,5]{1,0:T(8,128)(2,1)S(1)} %copy.57), kind=kOutput, calls=%fused_computation.24 | convolution fusion | flops 1781997568 | bytes 33653776 | tf_op jit(solution)/shard_map/ikab,ikbm->iam/dot_general | solution.py:127
  433.6 5.2 convert_element_type.146
  450.7 20.0 %gather_fusion.2 = bf16[520,128,104]{1,2,0:T(8,128)(2,1)} fusion(bf16[104,128,104]{1,2,0:T(8,128)(2,1)S(1)} %copy.74, s32[1024]{0:T(1024)S(1)} %pad_clamp_fusion), kind=kCustom, calls=%fused_computation.2 | custom fusion | bytes 27691040 | tf_op jit(solution)/shard_map/gather | solution.py:126
  470.7 13.1 %bitcast_convert_fusion.1 = bf16[104,128,104]{1,2,0:T(8,128)(2,1)S(1)} fusion(bf16[104,5,128,104]{2,3,1,0:T(8,128)(2,1)} %bitcast.114, bf16[104,5,128,128]{3,2,1,0:T(8,128)(2,1)} %param.6, bf16[104,5]{1,0:T(8,128)(2,1)S(1)} %copy.57), kind=kOutput, calls=%fused_computation.25 | convolution fusion | flops 1781997568 | bytes 33653776 | tf_op jit(solution)/shard_map/ikab,ikbm->iam/dot_general | solution.py:127
  485.7 6.4 convert_element_type.140
  492.5 5.9 all_to_all.101
  498.4 4.5 all-to-all-start.10
  505.5 17.1 %all-to-all-done.10 = bf16[8,832,1,104]{1,3,2,0:T(8,128)(2,1)} async-done(((bf16[8,832,1,104]{1,3,2,0:T(8,128)(2,1)}), bf16[8,832,1,104]{1,3,2,0:T(8,128)(2,1)}, u32[]{:S(2)}, u32[]{:S(2)}) %all-to-all-start.10) | async-done | bytes 1384480 | tf_op jit(solution)/shard_map/all_to_all | solution.py:58
  522.7 5.4 all-to-all-start.11
  528.1 4.7 copy.77
  532.7 15.1 %all-to-all-done.11 = bf16[8,832,1,104]{1,3,2,0:T(8,128)(2,1)} async-done(((bf16[8,832,1,104]{1,3,2,0:T(8,128)(2,1)}), bf16[8,832,1,104]{1,3,2,0:T(8,128)(2,1)}, u32[]{:S(2)}, u32[]{:S(2)}) %all-to-all-start.11) | async-done | bytes 1384480 | tf_op jit(solution)/shard_map/all_to_all | solution.py:58
  547.8 4.7 all-to-all-start.8
  552.6 5.1 maximum_convert_fusion.1
  557.7 31.5 %all-to-all-done.8 = bf16[8,2,832,1,104]{2,1,4,3,0:T(2,128)(2,1)S(1)} async-done(((bf16[8,2,832,1,104]{2,1,4,3,0:T(2,128)(2,1)}), bf16[8,2,832,1,104]{2,1,4,3,0:T(2,128)(2,1)S(1)}, u32[]{:S(2)}, u32[]{:S(2)}) %all-to-all-start.8) | async-done | bytes 2768928 | tf_op jit(solution)/shard_map/all_to_all | solution.py:35
  592.7 7.1 %copy.84 = f32[832,1664]{1,0:T(8,128)} copy(f32[832,1664]{0,1:T(8,128)} %bitcast.113) | data formatting | bytes 11075584 | tf_op jit(solution)/shard_map/convert_element_type | solution.py:167
  599.9 11.8 %multiply_reduce_fusion.1 = (f32[]{:T(128)}, f32[]{:T(128)}, f32[832,1664]{1,0:T(8,128)}) fusion(f32[832,1664]{1,0:T(8,128)} %get-tuple-element.9, f32[]{:T(128)S(6)} %max.13, bf16[832,1664]{1,0:T(8,128)(2,1)S(1)} %copy-done.1, f32[]{:T(128)} %sqrt.10, f32[832,1664]{1,0:T(8,128)} %get-tuple-element.19, f32[832,1664]{1,0:T(8,128)} %copy.84, ...), kind=kLoop, calls=%fused_computation.30 | loop fusion | flops 16613374 | bytes 30457872 | tf_op jit(solution)/shard_map/reduce_sum | solution.py:172
  613.7 28.7 %shard_map.78 = f32[8,128]{1,0:T(8,128)} custom-call(f32[8,128]{1,0:T(8,128)} %broadcast.41.x_ref), custom_call_target="tpu_custom_call" | custom-call | tf_op jit(solution)/shard_map/pallas_call | solution.py:106
  647.1 7.1 %divide_convert_fusion = bf16[832,1664]{1,0:T(8,128)(2,1)} fusion(f32[832,1664]{1,0:T(8,128)} %get-tuple-element.7, f32[832,1664]{1,0:T(8,128)} %get-tuple-element.9, f32[]{:T(128)} %sqrt.11, f32[]{:T(128)} %bitcast.41), kind=kLoop, calls=%fused_computation.28 | loop fusion | flops 5537792 | bytes 13844488 | tf_op jit(solution)/shard_map/convert_element_type | solution.py:181
  (59 shorter events, 75.4 us)
Async XLA Ops:
  35.1 11.0 %copy-start.4 = (s32[104,5]{0,1:T(8,128)S(1)}, s32[104,5]{0,1:T(8,128)}, u32[]{:S(2)}) copy-start(s32[104,5]{0,1:T(8,128)} %param.7) | copy-start | bytes 6244
  35.1 11.3 %copy-start.3 = (s32[104,5]{0,1:T(8,128)S(1)}, s32[104,5]{0,1:T(8,128)}, u32[]{:S(2)}) copy-start(s32[104,5]{0,1:T(8,128)} %param.8) | copy-start | bytes 6244
  35.1 39.0 %all-to-all-start.3 = ((bf16[1664,8,104]{0,2,1:T(8,128)(2,1)}), bf16[1664,8,104]{0,2,1:T(8,128)(2,1)S(1)}, u32[]{:S(2)}, u32[]{:S(2)}) async-start(bf16[1664,8,104]{0,2,1:T(8,128)(2,1)} %bitcast.11), calls=%async_computation.3 | async-start | bytes 5537792 | tf_op jit(solution)/shard_map/all_to_all | solution.py:161
  74.1 59.5 %all-to-all-start = ((bf16[832,16,104]{0,2,1:T(8,128)(2,1)}), bf16[832,16,104]{0,2,1:T(8,128)(2,1)}, u32[]{:S(2)}, u32[]{:S(2)}) async-start(bf16[832,16,104]{0,2,1:T(8,128)(2,1)} %bitcast.1), calls=%async_computation | async-start | bytes 5963776 | tf_op jit(solution)/shard_map/all_to_all | solution.py:155
  190.1 24.3 %all-to-all-start.4 = ((bf16[8,832,1,104]{1,3,2,0:T(8,128)(2,1)}), bf16[8,832,1,104]{1,3,2,0:T(8,128)(2,1)}, u32[]{:S(2)}, u32[]{:S(2)}) async-start(bf16[8,832,1,104]{1,3,2,0:T(8,128)(2,1)} %copy.69), calls=%async_computation.4 | async-start | bytes 2981888 | tf_op jit(solution)/shard_map/all_to_all | solution.py:58
  214.4 25.2 %all-to-all-start.5 = ((bf16[8,832,1,104]{1,3,2,0:T(8,128)(2,1)}), bf16[8,832,1,104]{1,3,2,0:T(8,128)(2,1)}, u32[]{:S(2)}, u32[]{:S(2)}) async-start(bf16[8,832,1,104]{1,3,2,0:T(8,128)(2,1)} %copy.70), calls=%async_computation.5 | async-start | bytes 2981888 | tf_op jit(solution)/shard_map/all_to_all | solution.py:58
  239.6 41.3 %all-to-all-start.2 = ((bf16[8,2,832,1,104]{2,1,4,3,0:T(2,128)(2,1)}), bf16[8,2,832,1,104]{2,1,4,3,0:T(2,128)(2,1)S(1)}, u32[]{:S(2)}, u32[]{:S(2)}) async-start(bf16[8,2,832,1,104]{2,1,4,3,0:T(2,128)(2,1)} %copy.64), calls=%async_computation.2 | async-start | bytes 5963776 | tf_op jit(solution)/shard_map/all_to_all | solution.py:35
  284.4 7.1 %copy-start = (bf16[832,1664]{1,0:T(8,128)(2,1)S(1)}, bf16[832,1664]{1,0:T(8,128)(2,1)}, u32[]{:S(2)}) copy-start(bf16[832,1664]{1,0:T(8,128)(2,1)} %param.5) | copy-start | bytes 8306692
  345.9 5.3 copy-start.2
  345.9 38.8 %all-to-all-start.9 = ((bf16[1664,8,104]{0,2,1:T(8,128)(2,1)}), bf16[1664,8,104]{0,2,1:T(8,128)(2,1)}, u32[]{:S(2)}, u32[]{:S(2)}) async-start(bf16[1664,8,104]{0,2,1:T(8,128)(2,1)} %bitcast.111), calls=%async_computation.9 | async-start | bytes 5537792 | tf_op jit(solution)/shard_map/all_to_all | solution.py:161
  384.6 57.3 %all-to-all-start.6 = ((bf16[832,16,104]{0,2,1:T(8,128)(2,1)}), bf16[832,16,104]{0,2,1:T(8,128)(2,1)}, u32[]{:S(2)}, u32[]{:S(2)}) async-start(bf16[832,16,104]{0,2,1:T(8,128)(2,1)} %bitcast.118), calls=%async_computation.6 | async-start | bytes 5963776 | tf_op jit(solution)/shard_map/all_to_all | solution.py:155
  498.4 24.3 %all-to-all-start.10 = ((bf16[8,832,1,104]{1,3,2,0:T(8,128)(2,1)}), bf16[8,832,1,104]{1,3,2,0:T(8,128)(2,1)}, u32[]{:S(2)}, u32[]{:S(2)}) async-start(bf16[8,832,1,104]{1,3,2,0:T(8,128)(2,1)} %copy.82), calls=%async_computation.10 | async-start | bytes 2981888 | tf_op jit(solution)/shard_map/all_to_all | solution.py:58
  522.7 25.2 %all-to-all-start.11 = ((bf16[8,832,1,104]{1,3,2,0:T(8,128)(2,1)}), bf16[8,832,1,104]{1,3,2,0:T(8,128)(2,1)}, u32[]{:S(2)}, u32[]{:S(2)}) async-start(bf16[8,832,1,104]{1,3,2,0:T(8,128)(2,1)} %copy.83), calls=%async_computation.11 | async-start | bytes 2981888 | tf_op jit(solution)/shard_map/all_to_all | solution.py:58
  547.8 41.3 %all-to-all-start.8 = ((bf16[8,2,832,1,104]{2,1,4,3,0:T(2,128)(2,1)}), bf16[8,2,832,1,104]{2,1,4,3,0:T(2,128)(2,1)S(1)}, u32[]{:S(2)}, u32[]{:S(2)}) async-start(bf16[8,2,832,1,104]{2,1,4,3,0:T(2,128)(2,1)} %copy.77), calls=%async_computation.8 | async-start | bytes 5963776 | tf_op jit(solution)/shard_map/all_to_all | solution.py:35
  592.7 7.1 %copy-start.1 = (bf16[832,1664]{1,0:T(8,128)(2,1)S(1)}, bf16[832,1664]{1,0:T(8,128)(2,1)}, u32[]{:S(2)}) copy-start(bf16[832,1664]{1,0:T(8,128)(2,1)} %param.5) | copy-start | bytes 8306692
